TPU v7x, 64 devices: a 2x2x8 block of a 4x4x8 slice. The times are simulated.
64 devices in a mesh: data: 4 (over x, y), ep: 16 (over z, core).
Axes of the slice: x: 2, y: 2, z: 8, core: 2. Of those that a mesh axis runs over, the one named last changes fastest.
The devices are a block of a 4x4x8 slice.
Arguments:
- x_in: bfloat16 [64, 384, 2048], P(('data', 'ep')), parts along dimension 0
- w_query: bfloat16 [2048, 16, 128], P('ep')
- w_keyval: bfloat16 [2048, 8, 128], P('ep')
- w_out: bfloat16 [2048, 2048], P('ep')
- attn_gain: bfloat16 [2048], replicated
- moe_gain: bfloat16 [2048], replicated
- w_gate: bfloat16 [64, 2048, 1408], P(None, 'ep')
- w_up: bfloat16 [64, 2048, 1408], P(None, 'ep')
- w_down: bfloat16 [64, 1408, 2048], P(None, None, 'ep')
- expert_ids: int32 [64, 384, 6], P(('data', 'ep')), parts along dimension 0
- slot_ids: int32 [64, 384, 6], P(('data', 'ep')), parts along dimension 0
- fill_counts: int32 [64, 64], P(('data', 'ep')), parts along dimension 0
- route_weight: bfloat16 [64, 384, 6], P(('data', 'ep')), parts along dimension 0
Outputs:
- output: bfloat16 [64, 384, 2048], P(('data', 'ep')), parts along dimension 0
There are 4 independent parts. A program takes and returns all parts, laid end to end along the dimension named above; an argument that names none is the same for every part.
All inputs are finite; a program needn't handle non-finite values.
Results may differ from a plain program's by a relative error of at most 0.02.
Values are sent between devices in bfloat16 or wider.
A program may use at most 768 MiB of HBM per device.

v0:
```python
import jax
import jax.numpy as jnp
from jax import lax
from jax.sharding import PartitionSpec as P


def rms_norm(val, gain):
    v32 = val.astype(jnp.float32)
    scale = lax.rsqrt(jnp.mean(v32 * v32, axis=-1, keepdims=True) + 1e-6)
    return (v32 * scale * gain.astype(jnp.float32)).astype(jnp.bfloat16)


def rotary(vals, cos_tab, sin_tab):
    half_dim = vals.shape[-1] // 2
    v32 = vals.astype(jnp.float32)
    first = v32[..., :half_dim]
    second = v32[..., half_dim:]
    return jnp.concatenate([first * cos_tab - second * sin_tab, second * cos_tab + first * sin_tab], axis=-1).astype(jnp.bfloat16)


def attention_block(x_in, w_query, w_keyval, w_out, attn_gain):
    batch_loc, seq_len, model_dim = x_in.shape
    num_heads, head_dim = w_query.shape[1], w_query.shape[2]
    kv_heads = w_keyval.shape[1] // 2
    groups = num_heads // kv_heads
    half_dim = head_dim // 2
    normed = rms_norm(x_in, attn_gain)
    query = jnp.einsum('bsd,dhk->bshk', normed, w_query, preferred_element_type=jnp.float32).astype(jnp.bfloat16)
    keyval = jnp.einsum('bsd,dhk->bshk', normed, w_keyval, preferred_element_type=jnp.float32).astype(jnp.bfloat16)
    inv_freq = 10000.0 ** (-jnp.arange(half_dim, dtype=jnp.float32) / half_dim)
    angles = jnp.arange(seq_len, dtype=jnp.float32)[:, None] * inv_freq[None, :]
    cos_tab = jnp.cos(angles)[None, :, None, :]
    sin_tab = jnp.sin(angles)[None, :, None, :]
    query = rotary(query, cos_tab, sin_tab).reshape(batch_loc, seq_len, kv_heads, groups, head_dim)
    keys = rotary(keyval[:, :, :kv_heads], cos_tab, sin_tab)
    values = keyval[:, :, kv_heads:]
    scores = jnp.einsum('bqhgk,bshk->bhgqs', query, keys, preferred_element_type=jnp.float32) * (head_dim ** -0.5)
    causal = jnp.arange(seq_len)[:, None] >= jnp.arange(seq_len)[None, :]
    scores = jnp.where(causal, scores, -1e30)
    attn_prob = jax.nn.softmax(scores, axis=-1).astype(jnp.bfloat16)
    mixed = jnp.einsum('bhgqs,bshk->bqhgk', attn_prob, values, preferred_element_type=jnp.float32).astype(jnp.bfloat16)
    attn_out = jnp.einsum('crg,ge->cre', mixed.reshape(batch_loc, seq_len, num_heads * head_dim), w_out, preferred_element_type=jnp.float32)
    return (x_in.astype(jnp.float32) + attn_out).astype(jnp.bfloat16)


def pack_rows(u_rows, ids, slots, counts, experts, capacity):
    tokens, choices = ids.shape
    count_at = jnp.take(counts.reshape(-1), ids)
    flat_pos = jnp.where(slots < count_at, ids * capacity + slots, experts * capacity)
    tok_ids = jnp.broadcast_to(jnp.arange(tokens, dtype=jnp.int32)[:, None], (tokens, choices))
    slot_owner = jnp.full((experts * capacity + 1,), tokens, jnp.int32).at[flat_pos.reshape(-1)].set(tok_ids.reshape(-1))
    packed = jnp.take(u_rows, slot_owner[:experts * capacity], axis=0, mode='fill', fill_value=0)
    return packed.reshape(experts, capacity, u_rows.shape[-1]), flat_pos


def combine_rows(h_rows, back, flat_pos, gate_rows):
    experts, capacity, model_dim = back.shape
    picked = jnp.take(back.reshape(experts * capacity, model_dim), flat_pos, axis=0, mode='fill', fill_value=0)
    mix_sum = jnp.einsum('tk,tkd->td', gate_rows, picked, preferred_element_type=jnp.float32)
    return (h_rows.astype(jnp.float32) + mix_sum).astype(jnp.bfloat16)


def expert_ffn(in_rows, w_gate, w_up, w_down):
    act_gate = jnp.einsum('ecd,edf->ecf', in_rows, w_gate, preferred_element_type=jnp.float32)
    act_up = jnp.einsum('ecd,edf->ecf', in_rows, w_up, preferred_element_type=jnp.float32)
    hidden_mid = (jax.nn.silu(act_gate) * act_up).astype(jnp.bfloat16)
    return jnp.einsum('ecf,efd->ecd', hidden_mid, w_down, preferred_element_type=jnp.float32).astype(jnp.bfloat16)


def solution(mesh):
    row_spec = P(('data', 'ep'))

    def device_step(x_in, w_query, w_keyval, w_out, attn_gain, moe_gain, w_gate, w_up, w_down, expert_ids, slot_ids, fill_counts, route_weight):
        full_query = lax.all_gather(w_query, 'ep', axis=0, tiled=True)
        full_keyval = lax.all_gather(w_keyval, 'ep', axis=0, tiled=True)
        full_out = lax.all_gather(w_out, 'ep', axis=0, tiled=True)
        hidden = attention_block(x_in, full_query, full_keyval, full_out, attn_gain)
        own_gate = lax.all_to_all(w_gate, 'ep', 0, 1, tiled=True)
        own_up = lax.all_to_all(w_up, 'ep', 0, 1, tiled=True)
        own_down = lax.all_to_all(w_down, 'ep', 0, 2, tiled=True)
        batch_loc, seq_len, model_dim = x_in.shape
        experts = w_gate.shape[0]
        choices = expert_ids.shape[-1]
        tokens = batch_loc * seq_len
        capacity = 2 * tokens * choices // experts
        h_rows = hidden.reshape(tokens, model_dim)
        u_rows = rms_norm(h_rows, moe_gain)
        packed, flat_pos = pack_rows(u_rows, expert_ids.reshape(tokens, choices), slot_ids.reshape(tokens, choices), fill_counts, experts, capacity)
        received = lax.all_to_all(packed, 'ep', 0, 1, tiled=True)
        result = expert_ffn(received, own_gate, own_up, own_down)
        back = lax.all_to_all(result, 'ep', 1, 0, tiled=True)
        out_rows = combine_rows(h_rows, back, flat_pos, route_weight.reshape(tokens, choices))
        return out_rows.reshape(batch_loc, seq_len, model_dim)

    in_specs = (row_spec, P('ep'), P('ep'), P('ep'), P(), P(), P(None, 'ep'), P(None, 'ep'), P(None, None, 'ep'), row_spec, row_spec, row_spec, row_spec)
    return jax.shard_map(device_step, mesh=mesh, in_specs=in_specs, out_specs=row_spec, check_vma=False)
```

profile of v0, /device:TPU:21, one launch (start us, length us, event | category | flops | bytes accessed | tf_op | source)
XLA Modules:
  0.0 2772.6 jit_solution(4144426164180047209)
XLA Ops:
  6.5 515.1 %all_to_all.87 = bf16[64,128,1408]{2,1,0:T(8,128)(2,1)} all-to-all(bf16[64,128,1408]{2,1,0:T(8,128)(2,1)} %param.19), channel_id=1, replica_groups=mesh['data'=4,'ep'=16] {'ep'}, dimensions={0} | all-to-all | bytes 46137344 | tf_op jit(solution)/shard_map/all_to_all | solution.py:78
  521.6 5.7 all-to-all-start.2
  527.5 0.9 copy.69
  528.5 539.2 %all-to-all-done.2 = bf16[64,128,1408]{2,1,0:T(8,128)(2,1)} async-done(((bf16[64,128,1408]{2,1,0:T(8,128)(2,1)}), bf16[64,128,1408]{2,1,0:T(8,128)(2,1)}, u32[]{:S(2)}, u32[]{:S(2)}) %all-to-all-start.2) | async-done | bytes 23068704 | tf_op jit(solution)/shard_map/all_to_all | solution.py:79
  1067.7 5.8 all-to-all-start.3
  1073.6 1.2 copy.70
  1075.0 0.7 all-gather.8.cloned.1.call-update
  1076.1 0.7 fusion.74
  1076.8 0.7 fusion.72
  1077.5 0.7 fusion.71
  1078.2 0.7 fusion.73
  1079.0 40.8 %compare_and_fusion.1 = (pred[384,6]{0,1:T(8,128)(4,1)}, s32[384,6]{0,1:T(8,128)S(1)}) fusion(s32[1,384,6]{1,0,2:T(1,128)S(1)} %copy-done.8, s32[1,384,6]{1,0,2:T(1,128)S(1)} %copy-done.12, s32[]{:T(128)} %bitcast.145, s32[]{:T(128)} %bitcast.144, s32[]{:T(128)} %bitcast.143, s32[]{:T(128)} %bitcast.142, s32[]{:T(128)} %bitcast.141, s32[]{:T(128)} %bitcast.140, ...), kind=kLoop, calls=%fused_computation.102 | loop fusion | flops 336384 | bytes 39424 | tf_op jit(solution)/shard_map/jit(_take)/and | solution.py:58
  1120.6 9.0 scatter_custom_fusion
  1129.8 0.4 fusion.10
  1130.3 0.4 fusion.37
  1130.7 4.6 fusion.30
  1135.6 215.9 %all-gather.6.cloned.1.call-done = bf16[2048,16,128]{0,2,1:T(8,128)(2,1)} async-done(((bf16[128,16,128]{0,2,1:T(8,128)(2,1)}), bf16[2048,16,128]{0,2,1:T(8,128)(2,1)}) %all-gather.6.cloned.1.call-update) | async-done | bytes 8388624 | tf_op jit(solution)/shard_map/all_gather | solution.py:74
  1351.5 8.0 fusion.28
  1359.7 0.5 subtract_convert_fusion
  1360.2 1.6 copy.71
  1361.8 1.5 copy.72
  1363.4 4.1 fusion.5
  1367.5 2.0 fusion.4
  1369.5 4.0 fusion.19
  1373.5 247.6 %all-gather.8.cloned.1.call-done = bf16[2048,2048]{1,0:T(8,128)(2,1)} async-done(((bf16[128,2048]{1,0:T(8,128)(2,1)}), bf16[2048,2048]{1,0:T(8,128)(2,1)}) %all-gather.8.cloned.1.call-update) | async-done | bytes 8388624 | tf_op jit(solution)/shard_map/all_gather | solution.py:76
  1621.1 7.7 fusion.14
  1628.8 1.1 copy-done.1
  1629.9 0.4 fusion.16
  1630.3 18.5 gather_fusion
  1648.8 16.8 broadcast_select_fusion
  1665.7 10.3 all-to-all-start
  1675.9 20.5 copy.84
  1696.4 20.4 copy.85
  1716.8 24.9 copy.141
  1741.7 34.3 %all_to_all.78 = bf16[4,1408,2048]{2,1,0:T(8,128)(2,1)} reshape(bf16[4,1408,16,128]{3,2,1,0:T(8,128)(2,1)} %bitcast.425) | data formatting | bytes 46137344 | tf_op jit(solution)/shard_map/all_to_all | solution.py:80
  1776.0 327.2 %all-to-all-done = bf16[64,72,2048]{2,1,0:T(8,128)(2,1)} async-done(((bf16[64,72,2048]{2,1,0:T(8,128)(2,1)}), bf16[64,72,2048]{2,1,0:T(8,128)(2,1)}, u32[]{:S(2)}, u32[]{:S(2)}) %all-to-all-start) | async-done | bytes 18874400 | tf_op jit(solution)/shard_map/all_to_all | solution.py:89
  2103.2 9.2 copy.83
  2112.4 39.9 %fusion.75 = f32[4,1152,1408]{2,1,0:T(8,128)} fusion(bf16[4,1152,2048]{2,1,0:T(8,128)(2,1)S(1)} %bitcast.429, bf16[4,2048,1408]{2,1,0:T(8,128)(2,1)} %bitcast.427), kind=kOutput, calls=%fused_computation.122 | convolution fusion | flops 26575110144 | bytes 67895296 | tf_op jit(solution)/shard_map/ecd,edf->ecf/dot_general | solution.py:64
  2152.3 42.9 %fusion.clone.4 = bf16[4,1152,1408]{2,1,0:T(8,128)(2,1)} fusion(bf16[4,1152,2048]{2,1,0:T(8,128)(2,1)} %bitcast.430, bf16[4,2048,1408]{2,1,0:T(8,128)(2,1)} %bitcast.428, f32[4,1152,1408]{2,1,0:T(8,128)} %fusion.75), kind=kOutput, calls=%fused_computation.5.clone.clone.clone.1 | convolution fusion | flops 26614038528 | bytes 80871424 | tf_op jit(solution)/shard_map/ecd,edf->ecf/dot_general | solution.py:65
  2195.2 38.7 %convolution_convert_fusion = bf16[4,1152,2048]{2,1,0:T(8,128)(2,1)} fusion(bf16[4,1408,2048]{2,1,0:T(8,128)(2,1)} %all_to_all.78, bf16[4,1152,1408]{2,1,0:T(8,128)(2,1)} %fusion.clone.4), kind=kOutput, calls=%fused_computation.4 | convolution fusion | flops 26584547328 | bytes 54919168 | tf_op jit(solution)/shard_map/ecf,efd->ecd/dot_general | solution.py:67
  2233.9 24.6 copy.87
  2258.6 7.4 all-to-all-start.4
  2266.8 426.1 %all-to-all-done.4 = bf16[4,1152,2048]{2,0,1:T(4,128)(2,1)} async-done(((bf16[4,1152,2048]{2,0,1:T(4,128)(2,1)}), bf16[4,1152,2048]{2,0,1:T(4,128)(2,1)}, u32[]{:S(2)}, u32[]{:S(2)}) %all-to-all-start.4) | async-done | bytes 18874400 | tf_op jit(solution)/shard_map/all_to_all | solution.py:91
  2692.9 20.8 copy.88
  2713.7 27.1 gather_fusion.1
  2740.8 15.7 reshape.497
  2756.5 6.7 fusion.1
  2763.3 2.3 fusion.22
  (72 shorter events, 2.9 us)
Async XLA Ops:
  521.6 5.8 copy-start.7
  521.6 546.1 %all-to-all-start.2 = ((bf16[64,128,1408]{2,1,0:T(8,128)(2,1)}), bf16[64,128,1408]{2,1,0:T(8,128)(2,1)}, u32[]{:S(2)}, u32[]{:S(2)}) async-start(bf16[64,128,1408]{2,1,0:T(8,128)(2,1)} %param.20), calls=%async_computation.2 | async-start | bytes 46137344 | tf_op jit(solution)/shard_map/all_to_all | solution.py:79
  527.4 603.3 %all-gather.4.cloned.1.call-start = ((), (), s32[]{:S(2)}) async-start(), calls=%async_computation.5 | async-start | bytes 4456448 | tf_op jit(solution)/shard_map/all_gather | solution.py:75
  528.4 545.2 %copy-start.6 = (bf16[128,16,128]{2,1,0:T(8,128)(2,1)S(1)}, bf16[128,16,128]{2,1,0:T(8,128)(2,1)}, u32[]{:S(2)}) copy-start(bf16[128,16,128]{2,1,0:T(8,128)(2,1)} %param.14) | copy-start | bytes 1572868
  528.4 547.3 %copy-start.16 = (bf16[2048]{0:T(1024)(128)(2,1)S(1)}, bf16[2048]{0:T(1024)(128)(2,1)}, u32[]{:S(2)}) copy-start(bf16[2048]{0:T(1024)(128)(2,1)} %param.17) | copy-start | bytes 12292
  528.5 547.3 %copy-start.17 = (bf16[2048]{0:T(1024)(128)(2,1)S(1)}, bf16[2048]{0:T(1024)(128)(2,1)}, u32[]{:S(2)}) copy-start(bf16[2048]{0:T(1024)(128)(2,1)} %param.18) | copy-start | bytes 12292
  528.5 547.3 %copy-start.12 = (s32[1,384,6]{1,0,2:T(1,128)S(1)}, s32[1,384,6]{1,0,2:T(1,128)}, u32[]{:S(2)}) copy-start(s32[1,384,6]{1,0,2:T(1,128)} %param.23) | copy-start | bytes 27652
  528.5 547.4 %copy-start.8 = (s32[1,384,6]{1,0,2:T(1,128)S(1)}, s32[1,384,6]{1,0,2:T(1,128)}, u32[]{:S(2)}) copy-start(s32[1,384,6]{1,0,2:T(1,128)} %param.22) | copy-start | bytes 27652
  528.5 547.6 %copy-start.3 = (s32[1,64]{1,0:T(1,128)S(1)}, s32[1,64]{1,0:T(1,128)}, u32[]{:S(2)}) copy-start(s32[1,64]{1,0:T(1,128)} %param.24) | copy-start | bytes 772
  528.5 601.3 %copy-start.4 = (bf16[1,384,2048]{2,1,0:T(8,128)(2,1)S(1)}, bf16[1,384,2048]{2,1,0:T(8,128)(2,1)}, u32[]{:S(2)}) copy-start(bf16[1,384,2048]{2,1,0:T(8,128)(2,1)} %param.13) | copy-start | bytes 4718596
  1067.7 598.0 %all-to-all-start.3 = ((bf16[64,1408,128]{2,1,0:T(8,128)(2,1)}), bf16[64,1408,128]{2,1,0:T(8,128)(2,1)}, u32[]{:S(2)}, u32[]{:S(2)}) async-start(bf16[64,1408,128]{2,1,0:T(8,128)(2,1)} %param.21), calls=%async_computation.3 | async-start | bytes 46137344 | tf_op jit(solution)/shard_map/all_to_all | solution.py:80
  1073.5 277.9 %all-gather.6.cloned.1.call-start = ((), (), s32[]{:S(2)}) async-start(), calls=%async_computation.6 | async-start | bytes 8912896 | tf_op jit(solution)/shard_map/all_gather | solution.py:74
  1074.9 546.2 %all-gather.8.cloned.1.call-start = ((), (), s32[]{:S(2)}) async-start(), calls=%async_computation.7 | async-start | bytes 8912896 | tf_op jit(solution)/shard_map/all_gather | solution.py:76
  1119.8 15.6 copy-start.10
  1369.5 251.6 %copy-start.5 = (bf16[1,384,2048]{2,1,0:T(8,128)(2,1)S(1)}, bf16[1,384,2048]{2,1,0:T(8,128)(2,1)}, u32[]{:S(2)}) copy-start(bf16[1,384,2048]{2,1,0:T(8,128)(2,1)} %param.13) | copy-start | bytes 4718596
  1628.8 1.1 copy-start.1
  1665.7 437.5 %all-to-all-start = ((bf16[64,72,2048]{2,1,0:T(8,128)(2,1)}), bf16[64,72,2048]{2,1,0:T(8,128)(2,1)}, u32[]{:S(2)}, u32[]{:S(2)}) async-start(bf16[64,72,2048]{2,1,0:T(8,128)(2,1)} %broadcast_select_fusion), calls=%async_computation | async-start | bytes 37748736 | tf_op jit(solution)/shard_map/all_to_all | solution.py:89
  2112.4 39.9 %copy-start = (bf16[4,16,72,2048]{3,2,1,0:T(8,128)(2,1)}, bf16[4,16,72,2048]{3,2,1,0:T(8,128)(2,1)S(1)}, u32[]{:S(2)}) copy-start(bf16[4,16,72,2048]{3,2,1,0:T(8,128)(2,1)S(1)} %copy.83) | copy-start | bytes 56623108
  2258.5 7.4 copy-start.9
  2258.5 7.5 copy-start.11
  2258.5 7.5 copy-start.13
  2258.5 7.8 copy-start.14
  2258.5 8.0 copy-start.15
  2258.6 434.3 %all-to-all-start.4 = ((bf16[4,1152,2048]{2,0,1:T(4,128)(2,1)}), bf16[4,1152,2048]{2,0,1:T(4,128)(2,1)}, u32[]{:S(2)}, u32[]{:S(2)}) async-start(bf16[4,1152,2048]{2,0,1:T(4,128)(2,1)} %copy.87), calls=%async_computation.4 | async-start | bytes 37748736 | tf_op jit(solution)/shard_map/all_to_all | solution.py:91
  2756.5 6.8 copy-start.2
Sparse Core Ops, SparseCore 0:
  529.8 165.8 all-gather.3
  1075.9 275.5 all-gather.5
  1353.1 267.9 all-gather.7
where the time goes:
time: 2780 us; the launch traced here: 2770 us
  waiting for transfers between devices  1760 us (63%)
  blocking collectives  515 us (19%)
  local copies, waits for them, and re-layouts  236 us (8%)
  matrix products  157 us (6%)
  other arithmetic  64.4 us (2%)
  starting transfers between devices  29.4 us (1%)
    all_to_all x1, waiting for transfers between devices, device_step(): own_up = lax.all_to_all(w_up, 'ep', 0, 1, tiled=True)  539 us
    all_to_all x1, blocking collectives, device_step(): own_gate = lax.all_to_all(w_gate, 'ep', 0, 1, tiled=True)  515 us
    all_to_all x1, waiting for transfers between devices, device_step(): back = lax.all_to_all(result, 'ep', 1, 0, tiled=True)  426 us
    all_to_all x1, waiting for transfers between devices, device_step(): received = lax.all_to_all(packed, 'ep', 0, 1, tiled=True)  327 us
    all_gather x1, waiting for transfers between devices, device_step(): full_out = lax.all_gather(w_out, 'ep', axis=0, tiled=True)  248 us
    all_gather x1, waiting for transfers between devices, device_step(): full_query = lax.all_gather(w_query, 'ep', axis=0, tiled=True)  216 us
    all_to_all x2, local copies, waits for them, and re-layouts, device_step(): own_down = lax.all_to_all(w_down, 'ep', 0, 2, tiled=True)  59.2 us
  transfers between devices with their start and end apart: 7, of which 5 were waited for; matrix products, arithmetic and copies ran while one was open for 7% of the time, Pallas kernels for 0%

commit v1 on v0

v1 whole, which is shorter than its diff:
```python
import functools
import math

import jax
import jax.numpy as jnp
from jax import lax
from jax.experimental import pallas as pl
from jax.experimental.pallas import tpu as pltpu
from jax.sharding import PartitionSpec as P

MESH = pl.DeviceIdType.MESH


def rms_norm(val, gain):
    v32 = val.astype(jnp.float32)
    scale = lax.rsqrt(jnp.mean(v32 * v32, axis=-1, keepdims=True) + 1e-6)
    return (v32 * scale * gain.astype(jnp.float32)).astype(jnp.bfloat16)


def rotary(vals, cos_tab, sin_tab):
    half_dim = vals.shape[-1] // 2
    v32 = vals.astype(jnp.float32)
    first = v32[..., :half_dim]
    second = v32[..., half_dim:]
    return jnp.concatenate([first * cos_tab - second * sin_tab, second * cos_tab + first * sin_tab], axis=-1).astype(jnp.bfloat16)


def attention_block(x_in, w_query, w_keyval, w_out, attn_gain):
    batch_loc, seq_len, model_dim = x_in.shape
    num_heads, head_dim = w_query.shape[1], w_query.shape[2]
    kv_heads = w_keyval.shape[1] // 2
    groups = num_heads // kv_heads
    half_dim = head_dim // 2
    normed = rms_norm(x_in, attn_gain)
    query = jnp.einsum('bsd,dhk->bshk', normed, w_query, preferred_element_type=jnp.float32).astype(jnp.bfloat16)
    keyval = jnp.einsum('bsd,dhk->bshk', normed, w_keyval, preferred_element_type=jnp.float32).astype(jnp.bfloat16)
    inv_freq = 10000.0 ** (-jnp.arange(half_dim, dtype=jnp.float32) / half_dim)
    angles = jnp.arange(seq_len, dtype=jnp.float32)[:, None] * inv_freq[None, :]
    cos_tab = jnp.cos(angles)[None, :, None, :]
    sin_tab = jnp.sin(angles)[None, :, None, :]
    query = rotary(query, cos_tab, sin_tab).reshape(batch_loc, seq_len, kv_heads, groups, head_dim)
    keys = rotary(keyval[:, :, :kv_heads], cos_tab, sin_tab)
    values = keyval[:, :, kv_heads:]
    scores = jnp.einsum('bqhgk,bshk->bhgqs', query, keys, preferred_element_type=jnp.float32) * (head_dim ** -0.5)
    causal = jnp.arange(seq_len)[:, None] >= jnp.arange(seq_len)[None, :]
    scores = jnp.where(causal, scores, -1e30)
    attn_prob = jax.nn.softmax(scores, axis=-1).astype(jnp.bfloat16)
    mixed = jnp.einsum('bhgqs,bshk->bqhgk', attn_prob, values, preferred_element_type=jnp.float32).astype(jnp.bfloat16)
    attn_out = jnp.einsum('crg,ge->cre', mixed.reshape(batch_loc, seq_len, num_heads * head_dim), w_out, preferred_element_type=jnp.float32)
    return (x_in.astype(jnp.float32) + attn_out).astype(jnp.bfloat16)


def exchange_kernel(n_ep, side, kinds, *refs):
    n = len(kinds)
    srcs, dsts = refs[:n], refs[n:2 * n]
    stage, s1_send, s1_recv, d_send, d_recv, f_send, f_recv, loc_sem = refs[2 * n:]
    dat, me = lax.axis_index('data'), lax.axis_index('ep')
    ybit = lax.rem(dat, 2)
    xbit = lax.rem(dat // side, 2)
    dat_y = dat + 1 - 2 * ybit
    dat_x = dat + side * (1 - 2 * xbit)
    place = 2 * xbit + ybit
    place_x = 2 * (1 - xbit) + ybit
    place_y = 2 * xbit + 1 - ybit
    per_dev = dsts[0].shape[0]
    chunks = [(m, j) for m in range(n) for j in range(per_dev)]

    barrier = pltpu.get_barrier_semaphore()

    @pl.loop(1, n_ep)
    def _(k):
        pl.semaphore_signal(barrier, inc=1, device_id=(dat, lax.rem(me + k, n_ep)), device_id_type=MESH)

    pl.semaphore_signal(barrier, inc=1, device_id=(dat_x, me), device_id_type=MESH)
    pl.semaphore_signal(barrier, inc=1, device_id=(dat_y, me), device_id_type=MESH)
    pl.semaphore_wait(barrier, n_ep + 1)

    def piece(m, j, owner, where):
        if kinds[m] == 'rows':
            rows = dsts[m].shape[2] // 4
            return dsts[m].at[j, owner, pl.ds(pl.multiple_of(where * rows, rows), rows), :]
        rows, cols = dsts[m].shape[1] // 4, dsts[m].shape[2] // n_ep
        return dsts[m].at[j, pl.ds(pl.multiple_of(where * rows, rows), rows), pl.ds(pl.multiple_of(owner * cols, cols), cols)]

    def quarter(m, j, where, part=None):
        if kinds[m] == 'rows':
            rows = dsts[m].shape[2] // 4
            who = pl.ds(0, n_ep) if part is None else pl.ds(part * (n_ep // 2), n_ep // 2)
            return dsts[m].at[j, who, pl.ds(pl.multiple_of(where * rows, rows), rows), :]
        rows, cols = dsts[m].shape[1] // 4, dsts[m].shape[2]
        who = pl.ds(0, cols) if part is None else pl.ds(part * (cols // 2), cols // 2)
        return dsts[m].at[j, pl.ds(pl.multiple_of(where * rows, rows), rows), who]

    def own_src(m, j, owner):
        rows = srcs[m].shape[1] // 4
        return srcs[m].at[owner * per_dev + j, pl.ds(pl.multiple_of(place * rows, rows), rows), :]

    def first(c, k):
        m, j = chunks[c]
        to, frm = lax.rem(me + k, n_ep), lax.rem(me - k + n_ep, n_ep)
        return pltpu.make_async_remote_copy(
            src_ref=own_src(m, j, to), dst_ref=piece(m, j, me, place), send_sem=s1_send.at[c, k], recv_sem=s1_recv.at[c, k],
            device_id=(dat, to), device_id_type=MESH)

    def direct(c, axis):
        m, j = chunks[c]
        ref = quarter(m, j, place)
        return pltpu.make_async_remote_copy(
            src_ref=ref, dst_ref=ref, send_sem=d_send.at[c, axis], recv_sem=d_recv.at[c, axis],
            device_id=(dat_x if axis == 0 else dat_y, me), device_id_type=MESH)

    def forward(c, axis):
        m, j = chunks[c]
        ref = quarter(m, j, place_y if axis == 0 else place_x, part=axis)
        return pltpu.make_async_remote_copy(
            src_ref=ref, dst_ref=ref, send_sem=f_send.at[c, axis], recv_sem=f_recv.at[c, axis],
            device_id=(dat_x if axis == 0 else dat_y, me), device_id_type=MESH)

    for c in range(len(chunks)):
        @pl.loop(1, n_ep)
        def _(k):
            first(c, k).start()

    for m in range(n):
        rows, cols = srcs[m].shape[1] // 4, srcs[m].shape[2]
        buf = stage[m]
        for j in range(per_dev):
            pltpu.make_async_copy(own_src(m, j, me), buf.at[j], loc_sem.at[m, j]).start()
    for m in range(n):
        buf = stage[m]
        for j in range(per_dev):
            pltpu.make_async_copy(own_src(m, j, me), buf.at[j], loc_sem.at[m, j]).wait()
            pltpu.make_async_copy(buf.at[j], piece(m, j, me, place), loc_sem.at[m, j]).start()
    for m in range(n):
        buf = stage[m]
        for j in range(per_dev):
            pltpu.make_async_copy(buf.at[j], piece(m, j, me, place), loc_sem.at[m, j]).wait()

    def pass_on(c):
        direct(c, 0).wait_recv()
        forward(c, 1).start()
        direct(c, 1).wait_recv()
        forward(c, 0).start()

    for c in range(len(chunks)):
        @pl.loop(1, n_ep)
        def _(k):
            first(c, k).wait_recv()

        direct(c, 0).start()
        direct(c, 1).start()
        if c > 0:
            pass_on(c - 1)
    pass_on(len(chunks) - 1)
    for c in range(len(chunks)):
        for axis in range(2):
            forward(c, axis).wait_recv()
            forward(c, axis).wait_send()
            direct(c, axis).wait_send()

        @pl.loop(1, n_ep)
        def _(k):
            first(c, k).wait_send()


def exchange(mats, kinds, n_ep, side, collective_id, cost):
    per_dev = mats[0].shape[0] // n_ep
    outs, stage = [], []
    for mat, kind in zip(mats, kinds):
        _, rows, cols = mat.shape
        outs.append((per_dev, n_ep, rows, cols) if kind == 'rows' else (per_dev, rows, cols * n_ep))
        stage.append(pltpu.VMEM((per_dev, rows // 4, cols), mat.dtype))
    n_chunks = len(mats) * per_dev
    dma = pltpu.SemaphoreType.DMA
    sent = sum(m.size * m.dtype.itemsize for m in mats)
    got = pl.pallas_call(
        functools.partial(exchange_kernel, n_ep, side, kinds),
        out_shape=[jax.ShapeDtypeStruct(o, m.dtype) for o, m in zip(outs, mats)],
        in_specs=[pl.BlockSpec(memory_space=pl.ANY)] * len(mats),
        out_specs=[pl.BlockSpec(memory_space=pl.ANY)] * len(mats),
        scratch_shapes=[stage, dma((n_chunks, n_ep)), dma((n_chunks, n_ep)), dma((n_chunks, 2)), dma((n_chunks, 2)),
                        dma((n_chunks, 2)), dma((n_chunks, 2)), dma((len(mats), per_dev))],
        compiler_params=pltpu.CompilerParams(collective_id=collective_id, has_side_effects=True),
        cost_estimate=pl.CostEstimate(flops=0, bytes_accessed=cost, transcendentals=0),
        name='exchange%d' % collective_id,
    )(*mats)
    return [g.reshape(g.shape[0], -1, g.shape[-1]) for g in got]


def slot_tables(ids, slots, counts, gates, experts, capacity):
    tokens, choices = ids.shape
    flat_ids, flat_slots = ids.reshape(-1), slots.reshape(-1)
    tok = jnp.repeat(jnp.arange(tokens, dtype=jnp.int32), choices)
    by_expert = (flat_ids[:, None] == jnp.arange(experts)[None, :]).astype(jnp.bfloat16)
    at_slot = (flat_slots[:, None] == jnp.arange(capacity)[None, :]).astype(jnp.bfloat16)
    cols = jnp.stack([(tok // 16).astype(jnp.bfloat16), (tok % 16).astype(jnp.bfloat16), gates.reshape(-1)], axis=1)
    spread = (at_slot[:, None, :] * cols[:, :, None]).reshape(tokens * choices, 3 * capacity)
    table = jnp.einsum('ne,nc->ec', by_expert, spread, preferred_element_type=jnp.float32).reshape(experts, 3, capacity)
    kept = jnp.arange(capacity)[None, :] < counts.reshape(-1)[:, None]
    owner = jnp.where(kept, table[:, 0] * 16 + table[:, 1], -1.0)
    gate = jnp.where(kept, table[:, 2], 0.0)
    return jnp.stack([owner, gate], axis=1)


def solution(mesh):
    row_spec = P(('data', 'ep'))
    n_ep = mesh.shape['ep']
    side = math.isqrt(mesh.shape['data'])

    def device_step(x_in, w_query, w_keyval, w_out, attn_gain, moe_gain, w_gate, w_up, w_down, expert_ids, slot_ids, fill_counts, route_weight):
        batch_loc, seq_len, model_dim = x_in.shape
        experts = w_gate.shape[0]
        per_dev = experts // n_ep
        choices = expert_ids.shape[-1]
        tokens = batch_loc * seq_len
        capacity = 2 * tokens * choices // experts
        full_query = lax.all_gather(w_query, 'ep', axis=0, tiled=True)
        full_keyval = lax.all_gather(w_keyval, 'ep', axis=0, tiled=True)
        full_out = lax.all_gather(w_out, 'ep', axis=0, tiled=True)
        (own_gate,) = exchange([w_gate], ['rows'], n_ep, side, 1, 400_000_000)
        x_in, own_gate = lax.optimization_barrier((x_in, own_gate))

        table = slot_tables(expert_ids.reshape(tokens, choices), slot_ids.reshape(tokens, choices), fill_counts, route_weight.reshape(tokens, choices), experts, capacity)
        table = lax.all_to_all(table, 'ep', 0, 1, tiled=True).reshape(per_dev, n_ep, 2, capacity)
        owner, gate = table[:, :, 0], table[:, :, 1]
        match = owner[..., None] == jnp.arange(tokens, dtype=jnp.float32)
        pick = match.astype(jnp.bfloat16)
        mix = jnp.where(match, gate[..., None], 0.0).astype(jnp.bfloat16)

        hidden = attention_block(x_in, full_query, full_keyval, full_out, attn_gain)
        h_rows = hidden.reshape(tokens, model_dim)
        u_rows = rms_norm(h_rows, moe_gain)
        all_u = lax.all_gather(u_rows, 'ep', axis=0)
        own_up, own_down = exchange([w_up, w_down], ['rows', 'cols'], n_ep, side, 2, 800_000_000)

        in_rows = jnp.einsum('esct,std->escd', pick, all_u, preferred_element_type=jnp.float32).astype(jnp.bfloat16)
        in_rows = in_rows.reshape(per_dev, n_ep * capacity, model_dim)
        act_gate = jnp.einsum('ecd,edf->ecf', in_rows, own_gate, preferred_element_type=jnp.float32)
        act_up = jnp.einsum('ecd,edf->ecf', in_rows, own_up, preferred_element_type=jnp.float32)
        hidden_mid = (jax.nn.silu(act_gate) * act_up).astype(jnp.bfloat16)
        y_rows = jnp.einsum('ecf,efd->ecd', hidden_mid, own_down, preferred_element_type=jnp.float32).astype(jnp.bfloat16)
        y_rows = y_rows.reshape(per_dev, n_ep, capacity, model_dim)
        partial = jnp.einsum('esct,escd->std', mix, y_rows, preferred_element_type=jnp.float32)
        total = lax.psum_scatter(partial, 'ep', scatter_dimension=0, tiled=False)
        out_rows = (h_rows.astype(jnp.float32) + total).astype(jnp.bfloat16)
        return out_rows.reshape(batch_loc, seq_len, model_dim)

    in_specs = (row_spec, P('ep'), P('ep'), P('ep'), P(), P(), P(None, 'ep'), P(None, 'ep'), P(None, None, 'ep'), row_spec, row_spec, row_spec, row_spec)
    return jax.shard_map(device_step, mesh=mesh, in_specs=in_specs, out_specs=row_spec, check_vma=False)
```

time: 2780 us -> 1220 us (0.44)
  waiting for transfers between devices: 1760 us -> 263 us
  Pallas kernels: 0 us -> 699 us
  blocking collectives: 515 us -> 0 us
  local copies, waits for them, and re-layouts: 236 us -> 20.6 us
  other arithmetic: 64.4 us -> 10.5 us
  matrix products: 157 us -> 195 us
    all_to_all x4 -> x1, waiting for transfers between devices: 1290 us -> 0.01 us  [device_step(): lax.all_to_all(table, 'ep', 0, 1, tiled=True)]
    pallas_call x0 -> x2, Pallas kernels: none -> 699 us  [exchange(): pl.pallas_call(functools.partial(exchange_kernel, n_ep, side, kinds), out...]
    all_to_all x1 -> x0, blocking collectives: 515 us -> none  [device_step(): own_gate = lax.all_to_all(w_gate, 'ep', 0, 1, tiled=True)]
    reduce_scatter x0 -> x1, waiting for transfers between devices: none -> 262 us  [device_step(): total = lax.psum_scatter(partial, 'ep', scatter_dimension=0, tiled=False)]
    all_gather x1, waiting for transfers between devices: 248 us -> 0.02 us  [device_step(): full_out = lax.all_gather(w_out, 'ep', axis=0, tiled=True)]
    all_gather x1, waiting for transfers between devices: 216 us -> 0.02 us  [device_step(): full_query = lax.all_gather(w_query, 'ep', axis=0, tiled=True)]
    all_to_all x6 -> x0, local copies, waits for them, and re-layouts: 130 us -> none  [the longest x2 59.2 us: device_step(): own_down = lax.all_to_all(w_down, 'ep', 0, 2, tiled=True)]
    gather x9 -> x0, local copies, waits for them, and re-layouts: 64.4 us -> none  [the longest x2 42.8 us: combine_rows(): jnp.take(back.reshape(experts * capacity, model_dim), flat_pos, axis=0, m...]
  transfers between devices with their start and end apart: 7 -> 6, of which waited for: 5 -> 1; matrix products, arithmetic and copies ran while one was open for 7% -> 3% of each run, Pallas kernels for 0% -> 58%
where the time goes in v1:
time: 1220 us; the launch traced here: 1210 us
  Pallas kernels  699 us (57%)
  waiting for transfers between devices  263 us (22%)
  matrix products  195 us (16%)
  local copies, waits for them, and re-layouts  20.6 us (2%)
  between operations  13.7 us (1%)
    pallas_call x2, Pallas kernels, exchange(): pl.pallas_call(functools.partial(exchange_kernel, n_ep, side, kinds), out...  699 us
    reduce_scatter x1, waiting for transfers between devices, device_step(): total = lax.psum_scatter(partial, 'ep', scatter_dimension=0, tiled=False)  262 us
    dot_general x1, matrix products, device_step(): jnp.einsum('ecd,edf->ecf', in_rows, own_up, preferred_element_type=jnp.fl...  43 us
    dot_general x1, matrix products, device_step(): jnp.einsum('ecd,edf->ecf', in_rows, own_gate, preferred_element_type=jnp....  39.8 us
    dot_general x1, matrix products, device_step(): jnp.einsum('ecf,efd->ecd', hidden_mid, own_down, preferred_element_type=j...  38.6 us
    dot_general x1, matrix products, device_step(): jnp.einsum('esct,escd->std', mix, y_rows, preferred_element_type=jnp.floa...  25.8 us
  transfers between devices with their start and end apart: 6, of which 1 were waited for; matrix products, arithmetic and copies ran while one was open for 3% of the time, Pallas kernels for 58%

profile of v1, /device:TPU:21, one launch (start us, length us, event | category | flops | bytes accessed | tf_op | source)
XLA Modules:
  0.0 1207.1 jit_solution(5197930485083290316)
XLA Ops:
  6.6 1.8 copy.32
  8.4 0.1 all-gather.7.cloned.1.call-start
  8.5 2.2 copy.33
  10.8 0.1 all-gather.9.cloned.1.call-start
  10.9 0.7 all-gather.9.cloned.1.call-update
  11.6 0.1 all-gather.11.cloned.1.call-start
  11.7 0.7 convert_element_type.116
  12.4 0.7 convert_element_type.134
  13.1 247.9 %exchange1.1 = bf16[4,16,128,1408]{3,2,1,0:T(8,128)(2,1)} custom-call(bf16[64,128,1408]{2,1,0:T(8,128)(2,1)} %refs_0_.2), custom_call_target="tpu_custom_call" | custom-call | bytes 400000000 | tf_op jit(solution)/shard_map/exchange1/pallas_call | solution.py:176
  261.1 0.4 fusion.19
  261.5 0.4 fusion.53
  261.9 4.6 fusion.45
  266.6 0.1 convert_bitcast_fusion.1
  266.7 0.1 fusion.50
  266.9 7.1 fusion.43
  274.0 0.2 bitcast_convert_fusion
  274.2 0.5 subtract_convert_fusion
  274.7 1.6 copy.35
  276.2 1.6 copy.34
  277.8 4.1 fusion.11
  281.9 2.0 fusion.10
  283.9 4.4 fusion.27
  288.3 7.7 fusion.23
  296.1 1.1 copy-done.1
  297.2 1.6 fusion.25
  298.8 0.2 copy.40
  299.0 0.2 stack_reshape_reshape.3
  299.2 0.1 copy.38
  299.4 0.1 eq.51
  299.5 0.1 copy.39
  299.7 0.1 eq.55
  299.8 0.2 reshape.377
  300.2 0.5 fusion.35
  300.7 0.1 fusion.54
  300.8 0.7 copy.41
  301.5 5.2 all-to-all-start
  306.7 0.1 reduce-scatter.2.cloned.1.call-start
  306.7 451.4 %exchange2.1 = (bf16[4,16,128,1408]{3,2,1,0:T(8,128)(2,1)}, bf16[4,1408,2048]{2,1,0:T(8,128)(2,1)}) custom-call(bf16[64,128,1408]{2,1,0:T(8,128)(2,1)} %refs_0_.3, bf16[64,1408,128]{2,1,0:T(8,128)(2,1)} %refs_1_.1), custom_call_target="tpu_custom_call" | custom-call | bytes 800000000 | tf_op jit(solution)/shard_map/exchange2/pallas_call | solution.py:176
  758.2 0.7 fusion.62
  758.8 0.6 copy-done.6
  759.4 19.1 %convert_bitcast_fusion = bf16[4,16,72,2048]{3,2,0,1:T(8,128)(2,1)} fusion(bf16[16,384,2048]{2,1,0:T(8,128)(2,1)} %all-gather.11.cloned.1.call-done, f32[4,16,72]{2,0,1:T(4,128)S(1)} %bitcast.117), kind=kOutput, calls=%fused_computation.7 | convolution fusion | flops 7258963968 | bytes 44058624 | tf_op jit(solution)/shard_map/esct,std->escd/dot_general | solution.py:236
  778.5 9.2 copy.42
  787.8 39.8 %fusion.63 = f32[4,1152,1408]{2,1,0:T(8,128)} fusion(bf16[4,1152,2048]{2,1,0:T(8,128)(2,1)S(1)} %bitcast.109, bf16[4,2048,1408]{2,1,0:T(8,128)(2,1)} %bitcast.108), kind=kOutput, calls=%fused_computation.95 | convolution fusion | flops 26575110144 | bytes 67895296 | tf_op jit(solution)/shard_map/ecd,edf->ecf/dot_general | solution.py:238
  827.6 43.0 %fusion.clone.4 = bf16[4,1152,1408]{2,1,0:T(8,128)(2,1)} fusion(bf16[4,1152,2048]{2,1,0:T(8,128)(2,1)} %bitcast.110, bf16[4,2048,1408]{2,1,0:T(8,128)(2,1)} %bitcast.120, f32[4,1152,1408]{2,1,0:T(8,128)} %fusion.63), kind=kOutput, calls=%fused_computation.2.clone.clone.clone.1 | convolution fusion | flops 26614038528 | bytes 80871424 | tf_op jit(solution)/shard_map/ecd,edf->ecf/dot_general | solution.py:239
  870.6 38.6 %convolution_convert_fusion = bf16[4,1152,2048]{2,1,0:T(8,128)(2,1)} fusion(bf16[4,1408,2048]{2,1,0:T(8,128)(2,1)} %get-tuple-element.12, bf16[4,1152,1408]{2,1,0:T(8,128)(2,1)} %fusion.clone.4), kind=kOutput, calls=%fused_computation.1 | convolution fusion | flops 26584547328 | bytes 54919168 | tf_op jit(solution)/shard_map/ecf,efd->ecd/dot_general | solution.py:241
  909.2 25.8 %fusion.5 = f32[16,384,2048]{2,1,0:T(8,128)} fusion(bf16[4,16,72,2048]{3,2,1,0:T(8,128)(2,1)} %bitcast.123, f32[4,16,72]{2,0,1:T(4,128)S(1)} %bitcast.116, f32[4,16,72]{2,0,1:T(4,128)S(1)} %bitcast.118), kind=kOutput, calls=%fused_computation.8 | convolution fusion | flops 7251296256 | bytes 69242880 | tf_op jit(solution)/shard_map/esct,escd->std/dot_general | solution.py:243
  935.1 261.8 %reduce-scatter.2.cloned.1.call-done = f32[1,384,2048]{2,1,0:T(8,128)} async-done(((f32[16,384,2048]{2,1,0:T(8,128)}), f32[1,384,2048]{2,1,0:T(8,128)}) %reduce-scatter.2.cloned.1.call-update) | async-done | bytes 3145744 | tf_op jit(solution)/shard_map/reduce_scatter | solution.py:244
  1196.9 3.5 fusion.26
  (43 shorter events, 0.7 us)
Async XLA Ops:
  6.5 255.4 %all-gather.5.cloned.1.call-start = ((), (), s32[]{:S(2)}) async-start(), calls=%async_computation.2 | async-start | bytes 4456448 | tf_op jit(solution)/shard_map/all_gather | solution.py:218
  8.4 258.4 %all-gather.7.cloned.1.call-start = ((), (), s32[]{:S(2)}) async-start(), calls=%async_computation.3 | async-start | bytes 8912896 | tf_op jit(solution)/shard_map/all_gather | solution.py:217
  10.8 277.5 %all-gather.9.cloned.1.call-start = ((), (), s32[]{:S(2)}) async-start(), calls=%async_computation.4 | async-start | bytes 8912896 | tf_op jit(solution)/shard_map/all_gather | solution.py:219
  11.6 747.2 %all-gather.11.cloned.1.call-start = ((), (), s32[]{:S(2)}) async-start(), calls=%async_computation.5 | async-start | bytes 26738688 | tf_op jit(solution)/shard_map/all_gather | solution.py:233
  13.1 248.0 %copy-start.3 = (bf16[1,384,2048]{2,1,0:T(8,128)(2,1)S(1)}, bf16[1,384,2048]{2,1,0:T(8,128)(2,1)}, u32[]{:S(2)}) copy-start(bf16[1,384,2048]{2,1,0:T(8,128)(2,1)} %param.13) | copy-start | bytes 4718596
  283.9 4.4 copy-start.4
  296.0 1.2 copy-start.1
  296.0 2.8 copy-start.10
  296.0 3.2 copy-start.8
  296.0 3.5 copy-start.9
  296.0 4.7 copy-start.11
  301.5 456.7 %all-to-all-start = ((f32[64,2,72]{2,1,0:T(2,128)}), f32[64,2,72]{2,1,0:T(2,128)S(1)}, u32[]{:S(2)}, u32[]{:S(2)}) async-start(f32[64,2,72]{2,1,0:T(2,128)} %copy.41), calls=%async_computation | async-start | bytes 131072 | tf_op jit(solution)/shard_map/all_to_all | solution.py:224
  306.7 890.2 %reduce-scatter.2.cloned.1.call-start = ((), (), s32[]{:S(2)}) async-start(), calls=%async_computation.6 | async-start | bytes 53477376 | tf_op jit(solution)/shard_map/reduce_scatter | solution.py:244
  758.8 0.6 copy-start.6
  787.8 39.9 %copy-start = (bf16[4,16,72,2048]{3,2,1,0:T(8,128)(2,1)}, bf16[4,16,72,2048]{3,2,1,0:T(8,128)(2,1)S(1)}, u32[]{:S(2)}) copy-start(bf16[4,16,72,2048]{3,2,1,0:T(8,128)(2,1)S(1)} %copy.42) | copy-start | bytes 56623108
  870.6 38.6 %copy-start.5 = (f32[4,16,1,72]{3,2,0,1:T(1,128)S(1)}, f32[4,16,1,72]{3,2,0,1:T(1,128)}, u32[]{:S(2)}) copy-start(f32[4,16,1,72]{3,2,0,1:T(1,128)} %get-tuple-element.21) | copy-start | bytes 55300
  870.6 38.6 %copy-start.7 = (f32[4,16,1,72]{3,2,0,1:T(1,128)S(1)}, f32[4,16,1,72]{3,2,0,1:T(1,128)}, u32[]{:S(2)}) copy-start(f32[4,16,1,72]{3,2,0,1:T(1,128)} %copy-done.6) | copy-start | bytes 55300
  935.0 261.8 %copy-start.2 = (bf16[1,384,2048]{2,1,0:T(8,128)(2,1)S(1)}, bf16[1,384,2048]{2,1,0:T(8,128)(2,1)}, u32[]{:S(2)}) copy-start(bf16[1,384,2048]{2,1,0:T(8,128)(2,1)} %copy-done.1) | copy-start | bytes 4718596
Sparse Core Ops, SparseCore 0:
  8.9 114.6 all-gather.4
  125.2 91.0 all-gather.6
  217.9 50.9 all-gather.8
  299.0 371.9 all-gather.10
  935.2 261.6 reduce-scatter.1

commit v2 on v1

--- a/solution.py
+++ b/solution.py
@@ -64,6 +64,12 @@
     place_y = 2 * xbit + 1 - ybit
     per_dev = dsts[0].shape[0]
     chunks = [(m, j) for m in range(n) for j in range(per_dev)]
+    parity = {'even': 0, 'odd': 1}
+
+    def only(m, owner):
+        if kinds[m] == 'rows':
+            return lambda step: step()
+        return pl.when(lax.rem(owner, 2) == parity[kinds[m]])
 
     barrier = pltpu.get_barrier_semaphore()
 
@@ -79,8 +85,8 @@
         if kinds[m] == 'rows':
             rows = dsts[m].shape[2] // 4
             return dsts[m].at[j, owner, pl.ds(pl.multiple_of(where * rows, rows), rows), :]
-        rows, cols = dsts[m].shape[1] // 4, dsts[m].shape[2] // n_ep
-        return dsts[m].at[j, pl.ds(pl.multiple_of(where * rows, rows), rows), pl.ds(pl.multiple_of(owner * cols, cols), cols)]
+        rows, cols = dsts[m].shape[1] // 4, srcs[m].shape[2]
+        return dsts[m].at[j, pl.ds(pl.multiple_of(where * rows, rows), rows), pl.ds(pl.multiple_of(owner // 2 * cols, cols), cols)]
 
     def quarter(m, j, where, part=None):
         if kinds[m] == 'rows':
@@ -117,24 +123,24 @@
             device_id=(dat_x if axis == 0 else dat_y, me), device_id_type=MESH)
 
     for c in range(len(chunks)):
-        @pl.loop(1, n_ep)
-        def _(k):
-            first(c, k).start()
-
-    for m in range(n):
-        rows, cols = srcs[m].shape[1] // 4, srcs[m].shape[2]
-        buf = stage[m]
-        for j in range(per_dev):
-            pltpu.make_async_copy(own_src(m, j, me), buf.at[j], loc_sem.at[m, j]).start()
+        @only(chunks[c][0], me)
+        def _():
+            @pl.loop(1, n_ep)
+            def _(k):
+                first(c, k).start()
+
     for m in range(n):
         buf = stage[m]
-        for j in range(per_dev):
-            pltpu.make_async_copy(own_src(m, j, me), buf.at[j], loc_sem.at[m, j]).wait()
-            pltpu.make_async_copy(buf.at[j], piece(m, j, me, place), loc_sem.at[m, j]).start()
-    for m in range(n):
-        buf = stage[m]
-        for j in range(per_dev):
-            pltpu.make_async_copy(buf.at[j], piece(m, j, me, place), loc_sem.at[m, j]).wait()
+
+        @only(m, me)
+        def _():
+            for j in range(per_dev):
+                pltpu.make_async_copy(own_src(m, j, me), buf.at[j], loc_sem.at[m, j]).start()
+            for j in range(per_dev):
+                pltpu.make_async_copy(own_src(m, j, me), buf.at[j], loc_sem.at[m, j]).wait()
+                pltpu.make_async_copy(buf.at[j], piece(m, j, me, place), loc_sem.at[m, j]).start()
+            for j in range(per_dev):
+                pltpu.make_async_copy(buf.at[j], piece(m, j, me, place), loc_sem.at[m, j]).wait()
 
     def pass_on(c):
         direct(c, 0).wait_recv()
@@ -145,7 +151,9 @@
     for c in range(len(chunks)):
         @pl.loop(1, n_ep)
         def _(k):
-            first(c, k).wait_recv()
+            @only(chunks[c][0], me - k + n_ep)
+            def _():
+                first(c, k).wait_recv()
 
         direct(c, 0).start()
         direct(c, 1).start()
@@ -158,9 +166,11 @@
             forward(c, axis).wait_send()
             direct(c, axis).wait_send()
 
-        @pl.loop(1, n_ep)
-        def _(k):
-            first(c, k).wait_send()
+        @only(chunks[c][0], me)
+        def _():
+            @pl.loop(1, n_ep)
+            def _(k):
+                first(c, k).wait_send()
 
 
 def exchange(mats, kinds, n_ep, side, collective_id, cost):
@@ -168,7 +178,7 @@
     outs, stage = [], []
     for mat, kind in zip(mats, kinds):
         _, rows, cols = mat.shape
-        outs.append((per_dev, n_ep, rows, cols) if kind == 'rows' else (per_dev, rows, cols * n_ep))
+        outs.append((per_dev, n_ep, rows, cols) if kind == 'rows' else (per_dev, rows, cols * n_ep // 2))
         stage.append(pltpu.VMEM((per_dev, rows // 4, cols), mat.dtype))
     n_chunks = len(mats) * per_dev
     dma = pltpu.SemaphoreType.DMA
@@ -231,17 +241,27 @@
         h_rows = hidden.reshape(tokens, model_dim)
         u_rows = rms_norm(h_rows, moe_gain)
         all_u = lax.all_gather(u_rows, 'ep', axis=0)
-        own_up, own_down = exchange([w_up, w_down], ['rows', 'cols'], n_ep, side, 2, 800_000_000)
+        own_up, down_even = exchange([w_up, w_down], ['rows', 'even'], n_ep, side, 2, 600_000_000)
 
         in_rows = jnp.einsum('esct,std->escd', pick, all_u, preferred_element_type=jnp.float32).astype(jnp.bfloat16)
         in_rows = in_rows.reshape(per_dev, n_ep * capacity, model_dim)
         act_gate = jnp.einsum('ecd,edf->ecf', in_rows, own_gate, preferred_element_type=jnp.float32)
         act_up = jnp.einsum('ecd,edf->ecf', in_rows, own_up, preferred_element_type=jnp.float32)
         hidden_mid = (jax.nn.silu(act_gate) * act_up).astype(jnp.bfloat16)
-        y_rows = jnp.einsum('ecf,efd->ecd', hidden_mid, own_down, preferred_element_type=jnp.float32).astype(jnp.bfloat16)
-        y_rows = y_rows.reshape(per_dev, n_ep, capacity, model_dim)
-        partial = jnp.einsum('esct,escd->std', mix, y_rows, preferred_element_type=jnp.float32)
-        total = lax.psum_scatter(partial, 'ep', scatter_dimension=0, tiled=False)
+
+        def weighted(down):
+            y_rows = jnp.einsum('ecf,efd->ecd', hidden_mid, down, preferred_element_type=jnp.float32).astype(jnp.bfloat16)
+            y_rows = y_rows.reshape(per_dev, n_ep, capacity, down.shape[-1])
+            return jnp.einsum('esct,escd->std', mix, y_rows, preferred_element_type=jnp.float32)
+
+        part_even = weighted(down_even)
+        w_down, part_even = lax.optimization_barrier((w_down, part_even))
+        sum_even = lax.psum_scatter(part_even, 'ep', scatter_dimension=0, tiled=False)
+        (down_odd,) = exchange([w_down], ['odd'], n_ep, side, 3, 400_000_000)
+        sum_odd = lax.psum_scatter(weighted(down_odd), 'ep', scatter_dimension=0, tiled=False)
+        block = w_down.shape[-1]
+        sums = [val.reshape(tokens, -1) for val in (sum_even, sum_odd)]
+        total = jnp.concatenate([val[:, at:at + block] for at in range(0, model_dim // 2, block) for val in sums], axis=1)
         out_rows = (h_rows.astype(jnp.float32) + total).astype(jnp.bfloat16)
         return out_rows.reshape(batch_loc, seq_len, model_dim)
 

time: 1220 us -> 1190 us (0.975)
  waiting for transfers between devices: 263 us -> 164 us
  Pallas kernels: 699 us -> 734 us
  local copies, waits for them, and re-layouts: 20.6 us -> 43.4 us
    reduce_scatter x1 -> x2, waiting for transfers between devices: 262 us -> 163 us  [the longest x1 139 us: device_step(): lax.psum_scatter(weighted(down_odd), 'ep', scatter_dimension=0, tiled=False)]
    pallas_call x2 -> x3, Pallas kernels: 699 us -> 734 us  [exchange(): pl.pallas_call(functools.partial(exchange_kernel, n_ep, side, kinds), out...]
    unnamed x29 -> x46, local copies, waits for them, and re-layouts: 6.3 us -> 27.4 us
    dot_general x2 -> x4, matrix products: 64.4 us -> 73.4 us  [the longest x2 44.9 us: weighted(): jnp.einsum('ecf,efd->ecd', hidden_mid, down, preferred_element_type=jnp.f...]
  transfers between devices with their start and end apart: 6 -> 7, of which waited for: 1 -> 2; matrix products, arithmetic and copies ran while one was open for 3% -> 6% of each run, Pallas kernels for 58% -> 62%
where the time goes in v2:
time: 1190 us; the launch traced here: 1180 us
  Pallas kernels  734 us (62%)
  matrix products  204 us (17%)
  waiting for transfers between devices  164 us (14%)
  local copies, waits for them, and re-layouts  43.4 us (4%)
  between operations  14.1 us (1%)
    pallas_call x3, Pallas kernels, exchange(): pl.pallas_call(functools.partial(exchange_kernel, n_ep, side, kinds), out...  734 us
    reduce_scatter x1, waiting for transfers between devices, device_step(): lax.psum_scatter(weighted(down_odd), 'ep', scatter_dimension=0, tiled=False)  139 us
    dot_general x2, matrix products, weighted(): jnp.einsum('ecf,efd->ecd', hidden_mid, down, preferred_element_type=jnp.f...  44.9 us
    dot_general x1, matrix products, device_step(): jnp.einsum('ecd,edf->ecf', in_rows, own_up, preferred_element_type=jnp.fl...  42.9 us
    dot_general x1, matrix products, device_step(): jnp.einsum('ecd,edf->ecf', in_rows, own_gate, preferred_element_type=jnp....  39.9 us
    dot_general x2, matrix products, weighted(): jnp.einsum('esct,escd->std', mix, y_rows, preferred_element_type=jnp.floa...  28.5 us
    unnamed x46, local copies, waits for them, and re-layouts  27.4 us
    reduce_scatter x1, waiting for transfers between devices, device_step(): lax.psum_scatter(part_even, 'ep', scatter_dimension=0, tiled=False)  24.1 us
  transfers between devices with their start and end apart: 7, of which 2 were waited for; matrix products, arithmetic and copies ran while one was open for 6% of the time, Pallas kernels for 62%

profile of v2, /device:TPU:21, one launch (start us, length us, event | category | flops | bytes accessed | tf_op | source)
XLA Modules:
  0.0 1175.5 jit_solution(9010234300681767032)
XLA Ops:
  6.6 1.8 copy.34
  8.5 2.2 copy.35
  10.9 0.7 all-gather.9.cloned.1.call-update
  11.7 0.7 convert_element_type.119
  12.4 0.7 convert_element_type.137
  13.1 247.8 %exchange1.1 = bf16[4,16,128,1408]{3,2,1,0:T(8,128)(2,1)} custom-call(bf16[64,128,1408]{2,1,0:T(8,128)(2,1)} %refs_0_.2), custom_call_target="tpu_custom_call" | custom-call | bytes 400000000 | tf_op jit(solution)/shard_map/exchange1/pallas_call | solution.py:186
  261.9 4.6 fusion.53
  266.8 7.1 fusion.51
  274.6 1.6 copy.37
  276.2 1.6 copy.36
  277.7 4.1 fusion.16
  281.9 2.0 fusion.15
  283.9 4.2 fusion.35
  288.1 7.7 fusion.31
  295.8 1.1 copy-done.1
  296.9 1.6 fusion.33
  300.5 0.7 copy.43
  301.2 5.3 all-to-all-start
  306.5 354.8 %exchange2.1 = (bf16[4,16,128,1408]{3,2,1,0:T(8,128)(2,1)}, bf16[4,1408,1024]{2,1,0:T(8,128)(2,1)}) custom-call(bf16[64,128,1408]{2,1,0:T(8,128)(2,1)} %refs_0_.3, bf16[64,1408,128]{2,1,0:T(8,128)(2,1)} %refs_0_.4), custom_call_target="tpu_custom_call" | custom-call | bytes 600000000 | tf_op jit(solution)/shard_map/exchange2/pallas_call | solution.py:186
  661.3 0.7 fusion.86
  662.6 19.5 %convert_bitcast_fusion = bf16[4,16,72,2048]{3,2,0,1:T(8,128)(2,1)} fusion(bf16[16,384,2048]{2,1,0:T(8,128)(2,1)} %all-gather.11.cloned.1.call-done, f32[4,16,72]{2,0,1:T(4,128)S(1)} %bitcast.199), kind=kOutput, calls=%fused_computation.4 | convolution fusion | flops 7258963968 | bytes 44058624 | tf_op jit(solution)/shard_map/esct,std->escd/dot_general | solution.py:246
  682.1 9.2 copy.44
  691.3 39.9 %fusion.87 = f32[4,1152,1408]{2,1,0:T(8,128)} fusion(bf16[4,1152,2048]{2,1,0:T(8,128)(2,1)S(1)} %bitcast.174, bf16[4,2048,1408]{2,1,0:T(8,128)(2,1)} %bitcast.173), kind=kOutput, calls=%fused_computation.134 | convolution fusion | flops 26575110144 | bytes 67895296 | tf_op jit(solution)/shard_map/ecd,edf->ecf/dot_general | solution.py:248
  731.2 42.9 %fusion = bf16[4,1152,1408]{2,1,0:T(8,128)(2,1)} fusion(bf16[4,1152,2048]{2,1,0:T(8,128)(2,1)} %bitcast.175, bf16[4,2048,1408]{2,1,0:T(8,128)(2,1)} %bitcast.203, f32[4,1152,1408]{2,1,0:T(8,128)} %fusion.87), kind=kOutput, calls=%fused_computation.1 | convolution fusion | flops 26614038528 | bytes 80871424 | tf_op jit(solution)/shard_map/ecd,edf->ecf/dot_general | solution.py:249
  774.1 22.4 %convolution_convert_fusion.1 = bf16[4,1152,1024]{2,1,0:T(8,128)(2,1)} fusion(bf16[4,1152,1408]{2,1,0:T(8,128)(2,1)} %fusion, bf16[4,1408,1024]{2,1,0:T(8,128)(2,1)} %get-tuple-element.14), kind=kOutput, calls=%fused_computation.6 | convolution fusion | flops 13292273664 | bytes 33947648 | tf_op jit(solution)/shard_map/ecf,efd->ecd/dot_general | solution.py:253
  796.6 14.4 %fusion.9 = f32[16,384,1024]{2,1,0:T(8,128)} fusion(bf16[4,16,72,1024]{3,2,1,0:T(8,128)(2,1)} %bitcast.207, f32[4,16,72]{2,0,1:T(4,128)S(1)} %bitcast.197, f32[4,16,72]{2,0,1:T(4,128)S(1)} %bitcast.200), kind=kOutput, calls=%fused_computation.14 | convolution fusion | flops 3627417600 | bytes 34639872 | tf_op jit(solution)/shard_map/esct,escd->std/dot_general | solution.py:255
  811.1 131.0 %exchange3.1 = bf16[4,1408,1024]{2,1,0:T(8,128)(2,1)} custom-call(bf16[64,1408,128]{2,1,0:T(8,128)(2,1)} %refs_0_.4), custom_call_target="tpu_custom_call" | custom-call | bytes 400000000 | tf_op jit(solution)/shard_map/exchange3/pallas_call | solution.py:186
  942.1 22.4 %convolution_convert_fusion = bf16[4,1152,1024]{2,1,0:T(8,128)(2,1)} fusion(bf16[4,1152,1408]{2,1,0:T(8,128)(2,1)} %fusion, bf16[4,1408,1024]{2,1,0:T(8,128)(2,1)} %exchange3.1), kind=kOutput, calls=%fused_computation.5 | convolution fusion | flops 13292273664 | bytes 33947648 | tf_op jit(solution)/shard_map/ecf,efd->ecd/dot_general | solution.py:253
  964.5 14.1 %fusion.12 = f32[16,384,1024]{2,1,0:T(8,128)} fusion(bf16[4,16,72,1024]{3,2,1,0:T(8,128)(2,1)} %bitcast.206, f32[4,16,72]{2,0,1:T(4,128)S(1)} %bitcast.198, f32[4,16,72]{2,0,1:T(4,128)S(1)} %bitcast.201), kind=kOutput, calls=%fused_computation.15 | convolution fusion | flops 3627417600 | bytes 34639872 | tf_op jit(solution)/shard_map/esct,escd->std/dot_general | solution.py:255
  978.7 24.1 %reduce-scatter.3.cloned.1.call-done = f32[1,384,1024]{2,1,0:T(8,128)} async-done(((f32[16,384,1024]{2,1,0:T(8,128)}), f32[1,384,1024]{2,1,0:T(8,128)}) %reduce-scatter.3.cloned.1.call-update) | async-done | bytes 1572880 | tf_op jit(solution)/shard_map/reduce_scatter | solution.py:259
  1002.9 1.8 fusion.75
  1004.6 139.3 %reduce-scatter.5.cloned.1.call-done = f32[1,384,1024]{2,1,0:T(8,128)} async-done(((f32[16,384,1024]{2,1,0:T(8,128)}), f32[1,384,1024]{2,1,0:T(8,128)}) %reduce-scatter.5.cloned.1.call-update) | async-done | bytes 1572880 | tf_op jit(solution)/shard_map/reduce_scatter | solution.py:261
  1143.9 1.7 fusion.74
  1145.6 1.7 fusion.73
  1147.2 1.6 fusion.72
  1148.9 1.7 fusion.71
  1150.5 1.6 fusion.70
  1152.2 1.6 fusion.69
  1153.8 1.6 fusion.68
  1155.4 0.7 fusion.67
  1156.2 1.6 fusion.66
  1157.8 0.7 fusion.65
  1158.6 1.6 fusion.64
  1160.2 0.7 fusion.63
  1160.9 1.6 fusion.62
  1162.5 0.7 fusion.61
  1163.3 1.6 fusion.60
  1164.9 3.5 fusion.34
  (67 shorter events, 5.0 us)
Async XLA Ops:
  6.5 255.3 %all-gather.5.cloned.1.call-start = ((), (), s32[]{:S(2)}) async-start(), calls=%async_computation.3 | async-start | bytes 4456448 | tf_op jit(solution)/shard_map/all_gather | solution.py:228
  8.5 258.3 %all-gather.7.cloned.1.call-start = ((), (), s32[]{:S(2)}) async-start(), calls=%async_computation.4 | async-start | bytes 8912896 | tf_op jit(solution)/shard_map/all_gather | solution.py:227
  10.8 277.3 %all-gather.9.cloned.1.call-start = ((), (), s32[]{:S(2)}) async-start(), calls=%async_computation.5 | async-start | bytes 8912896 | tf_op jit(solution)/shard_map/all_gather | solution.py:229
  11.6 650.3 %all-gather.11.cloned.1.call-start = ((), (), s32[]{:S(2)}) async-start(), calls=%async_computation.6 | async-start | bytes 26738688 | tf_op jit(solution)/shard_map/all_gather | solution.py:243
  13.1 247.9 %copy-start.3 = (bf16[1,384,2048]{2,1,0:T(8,128)(2,1)S(1)}, bf16[1,384,2048]{2,1,0:T(8,128)(2,1)}, u32[]{:S(2)}) copy-start(bf16[1,384,2048]{2,1,0:T(8,128)(2,1)} %param.13) | copy-start | bytes 4718596
  283.8 4.3 copy-start.4
  295.8 1.1 copy-start.1
  295.8 2.8 copy-start.11
  295.8 3.1 copy-start.9
  295.8 3.4 copy-start.10
  296.9 3.5 copy-start.12
  301.2 360.1 %all-to-all-start = ((f32[64,2,72]{2,1,0:T(2,128)}), f32[64,2,72]{2,1,0:T(2,128)S(1)}, u32[]{:S(2)}, u32[]{:S(2)}) async-start(f32[64,2,72]{2,1,0:T(2,128)} %copy.43), calls=%async_computation | async-start | bytes 131072 | tf_op jit(solution)/shard_map/all_to_all | solution.py:234
  306.5 696.4 %reduce-scatter.3.cloned.1.call-start = ((), (), s32[]{:S(2)}) async-start(), calls=%async_computation.7 | async-start | bytes 26738688 | tf_op jit(solution)/shard_map/reduce_scatter | solution.py:259
  662.0 0.6 copy-start.7
  691.3 39.9 %copy-start = (bf16[4,16,72,2048]{3,2,1,0:T(8,128)(2,1)}, bf16[4,16,72,2048]{3,2,1,0:T(8,128)(2,1)S(1)}, u32[]{:S(2)}) copy-start(bf16[4,16,72,2048]{3,2,1,0:T(8,128)(2,1)S(1)} %copy.44) | copy-start | bytes 56623108
  774.1 22.4 %copy-start.6 = (f32[4,16,1,72]{3,2,0,1:T(1,128)S(1)}, f32[4,16,1,72]{3,2,0,1:T(1,128)}, u32[]{:S(2)}) copy-start(f32[4,16,1,72]{3,2,0,1:T(1,128)} %get-tuple-element.25) | copy-start | bytes 55300
  774.1 22.4 %copy-start.8 = (f32[4,16,1,72]{3,2,0,1:T(1,128)S(1)}, f32[4,16,1,72]{3,2,0,1:T(1,128)}, u32[]{:S(2)}) copy-start(f32[4,16,1,72]{3,2,0,1:T(1,128)} %copy-done.7) | copy-start | bytes 55300
  811.0 332.9 %reduce-scatter.5.cloned.1.call-start = ((), (), s32[]{:S(2)}) async-start(), calls=%async_computation.8 | async-start | bytes 26738688 | tf_op jit(solution)/shard_map/reduce_scatter | solution.py:261
  1002.9 152.6 %copy-start.5 = (f32[1,384,1024]{2,1,0:T(8,128)S(1)}, f32[1,384,1024]{2,1,0:T(8,128)}, u32[]{:S(2)}) copy-start(f32[1,384,1024]{2,1,0:T(8,128)} %reduce-scatter.3.cloned.1.call-done) | copy-start | bytes 4718596
  1002.9 162.1 %copy-start.2 = (bf16[1,384,2048]{2,1,0:T(8,128)(2,1)S(1)}, bf16[1,384,2048]{2,1,0:T(8,128)(2,1)}, u32[]{:S(2)}) copy-start(bf16[1,384,2048]{2,1,0:T(8,128)(2,1)} %copy-done.1) | copy-start | bytes 4718596
Sparse Core Ops, SparseCore 0:
  8.9 115.3 all-gather.4
  125.8 90.6 all-gather.6
  218.2 51.0 all-gather.8
  298.7 311.3 all-gather.10
  811.1 191.6 reduce-scatter.2
  1005.1 138.7 reduce-scatter.4
